TPU v7x, 256 devices: a whole 4x4x8 slice. The times are simulated.
256 devices in a mesh: row: 8 (over z_lo, y), col: 32 (over z_hi, x, core).
Axes of the slice: x: 4, y: 4, z: 8 (z_hi: 4, z_lo: 2; z = z_hi * 2 + z_lo), core: 2. Of those that a mesh axis runs over, the one named last changes fastest.
Arguments:
- alignment: float32 [512, 768, 256], P('row', 'col'), may hold values from -40 to 40
- seq_mask: int32 [512], replicated, may hold values 0 or 1
- res_mask: int32 [768], replicated, may hold values 0 or 1
- attn_gain: float32 [256], replicated, may hold values from 0.5 to 1.5
- outer_product_gain: float32 [256], replicated, may hold values from 0.5 to 1.5
- w_query: bfloat16 [256, 256], replicated, may hold values from -24 to 24
- w_key: bfloat16 [256, 256], replicated, may hold values from -2 to 2
- w_value: bfloat16 [256, 256], replicated, may hold values from -0.375 to 0.375
- w_gate: bfloat16 [256, 256], replicated, may hold values from -0.375 to 0.375
- output_weight: bfloat16 [256, 256], replicated, may hold values from -0.375 to 0.375
- w_left: bfloat16 [256, 32], replicated, may hold values from -0.375 to 0.375
- w_right: bfloat16 [256, 32], replicated, may hold values from -0.375 to 0.375
- w_pair: bfloat16 [1024, 128], replicated, may hold values from -3 to 3
Outputs:
- alignment_output: float32 [512, 768, 256], P('row', 'col')
- pair_increment: float32 [768, 768, 128], P('row', 'col')
All inputs are finite; a program needn't handle non-finite values.
Results may differ from a plain program's by a relative error of at most 0.0095.
Values may be sent and summed in bfloat16 or wider, within the bound.
No kernel may reach another device: no remote copies, remote signals or barrier semaphores. Data moves between devices by JAX's collectives and lax.ppermute only.
A program may use at most 128 MiB of HBM per device.

v0:
```python
import jax
import jax.numpy as jnp
from jax import lax
from jax.sharding import PartitionSpec as P

HEADS = 8
HEAD_DIM = 32


def sent_to_all(shard, axis):
    copies = jnp.broadcast_to(shard, (lax.axis_size(axis), *shard.shape))
    return lax.all_to_all(copies, axis, split_axis=0, concat_axis=0, tiled=True)


def laid_out(blocks, dim):
    blocks = jnp.moveaxis(blocks, 0, dim)
    shape = blocks.shape
    return blocks.reshape(*shape[:dim], shape[dim] * shape[dim + 1], *shape[dim + 2 :])


def gathered_copies(shard, axis, dim):
    blocks = sent_to_all(shard, axis)
    return laid_out(blocks, dim)


def normalized_rows(values, gains):
    average = jnp.mean(values, -1, keepdims=True)
    centred = values - average
    spread = jnp.mean(centred * centred, -1, keepdims=True)
    return centred * lax.rsqrt(spread + 1e-05) * gains


def shards(
    alignment,
    seq_mask,
    res_mask,
    attn_gain,
    outer_product_gain,
    w_query,
    w_key,
    w_value,
    w_gate,
    output_weight,
    w_left,
    w_right,
    w_pair,
):
    seq_dev, res_dev, channel_width = alignment.shape
    row_count = lax.axis_size("row")
    col_count = lax.axis_size("col")
    sequence_total = seq_mask.shape[0]
    hidden = w_query.shape[1]
    query_scale = HEAD_DIM ** (-0.5)
    key_bias = jnp.where(seq_mask > 0, 0.0, -1000000000.0).astype(jnp.float32)
    normed = normalized_rows(alignment, attn_gain).astype(jnp.bfloat16)
    normed = normed.reshape(seq_dev, row_count, res_dev // row_count, channel_width)

    def column(column_parts):
        col_query, col_key, col_value, col_gate = column_parts
        heads_query = col_query.reshape(sequence_total, HEADS, HEAD_DIM)
        heads_key = col_key.reshape(sequence_total, HEADS, HEAD_DIM)
        heads_value = col_value.reshape(sequence_total, HEADS, HEAD_DIM)
        logits = (
            jnp.einsum("shd,thd->hst", heads_query, heads_key, preferred_element_type=jnp.float32)
            + key_bias[None, None, :]
        )
        weights = jax.nn.softmax(logits, axis=-1).astype(jnp.bfloat16)
        attended = jnp.einsum(
            "hst,thd->shd", weights, heads_value, preferred_element_type=jnp.float32
        ).reshape(sequence_total, hidden)
        return (jax.nn.sigmoid(col_gate) * attended).astype(jnp.bfloat16)

    tokens = lax.all_to_all(normed, "row", split_axis=1, concat_axis=0, tiled=True)[:, 0]
    residues = tokens.shape[1]
    token_rows = tokens.reshape(-1, channel_width)
    queries = (
        jnp.dot(token_rows, w_query, preferred_element_type=jnp.float32) * query_scale
    ).astype(jnp.bfloat16)
    key_rows = jnp.dot(token_rows, w_key, preferred_element_type=jnp.float32).astype(jnp.bfloat16)
    value_rows = jnp.dot(token_rows, w_value, preferred_element_type=jnp.float32).astype(
        jnp.bfloat16
    )
    gate_lin = jnp.dot(token_rows, w_gate, preferred_element_type=jnp.float32)

    def arrange(values):
        return values.reshape(sequence_total, residues, -1).transpose(1, 0, 2)

    gated_output = lax.map(
        column, (arrange(queries), arrange(key_rows), arrange(value_rows), arrange(gate_lin))
    )
    gated_output = gated_output.transpose(1, 0, 2)[:, None]
    returned_value = lax.all_to_all(gated_output, "row", split_axis=0, concat_axis=1, tiled=True)
    returned_value = returned_value.reshape(-1, hidden)
    alignment_output = alignment + jnp.dot(
        returned_value, output_weight, preferred_element_type=jnp.float32
    ).reshape(seq_dev, res_dev, channel_width)
    row_index = lax.axis_index("row")
    col_index = lax.axis_index("col")
    side_width = w_left.shape[1]
    second_normalized = (
        normalized_rows(alignment_output, outer_product_gain)
        .astype(jnp.bfloat16)
        .reshape(-1, channel_width)
    )
    own_seq = lax.dynamic_slice_in_dim(seq_mask, row_index * seq_dev, seq_dev, 0)
    own_res = lax.dynamic_slice_in_dim(res_mask, col_index * res_dev, res_dev, 0)
    side_mask = (own_seq[:, None] * own_res[None, :]).astype(jnp.float32)[:, :, None]
    left = (
        (
            jnp.dot(second_normalized, w_left, preferred_element_type=jnp.float32).reshape(
                seq_dev, res_dev, side_width
            )
            * side_mask
        )
        .astype(jnp.bfloat16)
        .reshape(seq_dev, -1)
    )
    right = (
        (
            jnp.dot(second_normalized, w_right, preferred_element_type=jnp.float32).reshape(
                seq_dev, res_dev, side_width
            )
            * side_mask
        )
        .astype(jnp.bfloat16)
        .reshape(seq_dev, -1)
    )
    pair_rows = res_dev * col_count // row_count
    contraction = (((0,), (0,)), ((), ()))
    right_all = gathered_copies(right, "row", 0)
    group = seq_dev // col_count
    right_order = (
        right_all.reshape(row_count, col_count, group, -1)
        .transpose(1, 0, 2, 3)
        .reshape(sequence_total, -1)
    )
    spread_out = lax.all_to_all(left, "col", split_axis=0, concat_axis=1, tiled=True)
    own_block = lax.all_to_all(spread_out, "row", split_axis=1, concat_axis=0, tiled=True)
    products = lax.dot_general(
        lax.all_gather(own_block, "col", axis=0, tiled=True),
        right_order,
        contraction,
        preferred_element_type=jnp.float32,
    )
    outer_sum = (
        products.reshape(pair_rows, side_width, res_dev, side_width)
        .transpose(0, 2, 1, 3)
        .reshape(-1, side_width * side_width)
        .astype(jnp.bfloat16)
    )
    projected_output = jnp.dot(outer_sum, w_pair, preferred_element_type=jnp.float32).reshape(
        pair_rows, res_dev, -1
    )
    pair_res = lax.dynamic_slice_in_dim(res_mask, row_index * pair_rows, pair_rows, 0)
    live_total = jnp.sum(seq_mask)
    count_values = jnp.maximum(live_total * pair_res[:, None] * own_res[None, :], 1).astype(
        jnp.float32
    )
    return (alignment_output, projected_output / count_values[:, :, None])


def solution(mesh):
    in_specs = (P("row", "col", None), P(), P(), P(), P(), P(), P(), P(), P(), P(), P(), P(), P())
    out_specs = (P("row", "col", None), P("row", "col", None))
    return jax.shard_map(shards, mesh=mesh, in_specs=in_specs, out_specs=out_specs, check_vma=False)
```

profile of v0, /device:TPU:5, one launch (start us, length us, event | category | flops | bytes accessed | tf_op | source)
XLA Modules:
  0.0 247.4 jit_solution(861617664489180695)
XLA Ops:
  11.4 5.5 %all-to-all-start = ((bf16[64,8,3,256]{3,0,2,1:T(8,128)(2,1)}), bf16[64,8,3,256]{3,0,2,1:T(8,128)(2,1)S(1)}, u32[]{:S(2)}, u32[]{:S(2)}) async-start(bf16[64,8,3,256]{3,0,2,1:T(8,128)(2,1)} %bitcast.5), calls=%async_computation | async-start | bytes 1572864 | tf_op jit(solution)/shard_map/all_to_all | solution.py:73
  17.0 11.5 %all-to-all-done = bf16[64,8,3,256]{3,0,2,1:T(8,128)(2,1)S(1)} async-done(((bf16[64,8,3,256]{3,0,2,1:T(8,128)(2,1)}), bf16[64,8,3,256]{3,0,2,1:T(8,128)(2,1)S(1)}, u32[]{:S(2)}, u32[]{:S(2)}) %all-to-all-start) | async-done | bytes 786464 | tf_op jit(solution)/shard_map/all_to_all | solution.py:73
  31.1 2.4 reshape_squeeze.3
  42.5 2.5 reshape.159
  46.6 2.6 %convolution_bitcast_fusion = f32[3,512,256]{2,1,0:T(8,128)} fusion(bf16[512,3,256]{2,0,1:T(8,128)(2,1)} %bitcast.103, bf16[256,256]{1,0:T(8,128)(2,1)S(1)} %copy-done.3), kind=kOutput, calls=%fused_computation.25 | convolution fusion | flops 201326592 | bytes 2490368 | tf_op jit(solution)/shard_map/dot_general | solution.py:83
  49.2 40.3 %while.10 = (s32[]{:T(128)}, bf16[3,512,256]{1,2,0:T(8,128)(2,1)}, f32[3,512,256]{2,1,0:T(8,128)}, bf16[3,512,256]{1,2,0:T(8,128)(2,1)}, bf16[3,512,256]{1,2,0:T...) while((s32[]{:T(128)}, bf16[3,512,256]{1,2,0:T(8,128)(2,1)}, ...), condition=%wide.region_5.6_spmd, body=%wide.region_2.5_spmd.sunk | while | flops 279577088 | bytes 23104096 | solution.py:88
  50.3 5.0 %fusion.43 = (f32[8,512]{1,0:T(8,128)S(1)}, f32[8,512,512]{1,2,0:T(8,128)}) fusion(f32[512]{0:T(512)S(1)} %get-tuple-element.174, bf16[512,8,32]{0,2,1:T(8,128)(2,1)S(1)} %bitcast.97, bf16[512,8,32]{0,2,1:T(8,128)(2,1)S(1)} %bitcast.96), kind=kOutput, calls=%fused_computation.46.clone.1 | convolution fusion | flops 140509696 | bytes 8931328 | tf_op jit(solution)/shard_map/while/body/eval_jaxpr/sub | solution.py:67
  56.3 4.2 %fusion.44 = f32[8,32,512]{2,1,0:T(8,128)S(1)} fusion(bf16[512,8,32]{0,2,1:T(8,128)(2,1)S(1)} %bitcast.95, f32[8,512,512]{1,2,0:T(8,128)} %get-tuple-element.150, f32[8,512]{1,0:T(8,128)S(1)} %get-tuple-element.151), kind=kOutput, calls=%fused_computation.6.clone.1 | convolution fusion | flops 138412032 | bytes 9191424 | tf_op jit(solution)/shard_map/while/body/eval_jaxpr/hst,thd->shd/dot_general | solution.py:68
  63.7 5.0 %fusion.43 = (f32[8,512]{1,0:T(8,128)S(1)}, f32[8,512,512]{1,2,0:T(8,128)}) fusion(f32[512]{0:T(512)S(1)} %get-tuple-element.174, bf16[512,8,32]{0,2,1:T(8,128)(2,1)S(1)} %bitcast.97, bf16[512,8,32]{0,2,1:T(8,128)(2,1)S(1)} %bitcast.96), kind=kOutput, calls=%fused_computation.46.clone.1 | convolution fusion | flops 140509696 | bytes 8931328 | tf_op jit(solution)/shard_map/while/body/eval_jaxpr/sub | solution.py:67
  69.7 4.2 %fusion.44 = f32[8,32,512]{2,1,0:T(8,128)S(1)} fusion(bf16[512,8,32]{0,2,1:T(8,128)(2,1)S(1)} %bitcast.95, f32[8,512,512]{1,2,0:T(8,128)} %get-tuple-element.150, f32[8,512]{1,0:T(8,128)S(1)} %get-tuple-element.151), kind=kOutput, calls=%fused_computation.6.clone.1 | convolution fusion | flops 138412032 | bytes 9191424 | tf_op jit(solution)/shard_map/while/body/eval_jaxpr/hst,thd->shd/dot_general | solution.py:68
  77.1 5.0 %fusion.43 = (f32[8,512]{1,0:T(8,128)S(1)}, f32[8,512,512]{1,2,0:T(8,128)}) fusion(f32[512]{0:T(512)S(1)} %get-tuple-element.174, bf16[512,8,32]{0,2,1:T(8,128)(2,1)S(1)} %bitcast.97, bf16[512,8,32]{0,2,1:T(8,128)(2,1)S(1)} %bitcast.96), kind=kOutput, calls=%fused_computation.46.clone.1 | convolution fusion | flops 140509696 | bytes 8931328 | tf_op jit(solution)/shard_map/while/body/eval_jaxpr/sub | solution.py:67
  83.1 4.2 %fusion.44 = f32[8,32,512]{2,1,0:T(8,128)S(1)} fusion(bf16[512,8,32]{0,2,1:T(8,128)(2,1)S(1)} %bitcast.95, f32[8,512,512]{1,2,0:T(8,128)} %get-tuple-element.150, f32[8,512]{1,0:T(8,128)S(1)} %get-tuple-element.151), kind=kOutput, calls=%fused_computation.6.clone.1 | convolution fusion | flops 138412032 | bytes 9191424 | tf_op jit(solution)/shard_map/while/body/eval_jaxpr/hst,thd->shd/dot_general | solution.py:68
  89.5 2.3 copy.104
  91.8 4.3 %all-to-all-start.1 = ((bf16[512,1,3,256]{3,2,1,0:T(4,128)(2,1)}), bf16[512,1,3,256]{3,2,1,0:T(4,128)(2,1)S(1)}, u32[]{:S(2)}, u32[]{:S(2)}) async-start(bf16[512,1,3,256]{3,2,1,0:T(4,128)(2,1)} %bitcast.102), calls=%async_computation.1 | async-start | bytes 2097152 | tf_op jit(solution)/shard_map/all_to_all | solution.py:92
  97.0 14.0 %all-to-all-done.1 = bf16[512,1,3,256]{3,2,1,0:T(4,128)(2,1)S(1)} async-done(((bf16[512,1,3,256]{3,2,1,0:T(4,128)(2,1)}), bf16[512,1,3,256]{3,2,1,0:T(4,128)(2,1)S(1)}, u32[]{:S(2)}, u32[]{:S(2)}) %all-to-all-start.1) | async-done | bytes 786464 | tf_op jit(solution)/shard_map/all_to_all | solution.py:92
  114.8 19.5 %all_to_all.70 = bf16[32,2,768]{2,1,0:T(2,128)(2,1)S(1)} all-to-all(bf16[32,2,768]{2,1,0:T(2,128)(2,1)S(1)} %all_to_all.57), channel_id=1, replica_groups=mesh['row'=8,'col'=32] {'col'}, dimensions={0} | all-to-all | bytes 196608 | tf_op jit(solution)/shard_map/all_to_all | solution.py:137
  134.3 8.1 %all_to_all.71 = bf16[2,8,3072]{2,0,1:T(2,128)(2,1)S(1)} all-to-all(bf16[2,8,3072]{2,0,1:T(2,128)(2,1)S(1)} %bitcast.112), channel_id=1, replica_groups=mesh['row'=8,'col'=32] {'row'}, dimensions={1} | all-to-all | bytes 196608 | tf_op jit(solution)/shard_map/all_to_all | solution.py:138
  145.3 3.5 %all-to-all-start.4 = ((bf16[8,64,768]{2,1,0:T(8,128)(2,1)}), bf16[8,64,768]{2,1,0:T(8,128)(2,1)S(1)}, u32[]{:S(2)}, u32[]{:S(2)}) async-start(bf16[8,64,768]{2,1,0:T(8,128)(2,1)} %broadcast_in_dim.23), calls=%async_computation.4 | async-start | bytes 1572864 | tf_op jit(solution)/shard_map/all_to_all | solution.py:12
  151.0 8.0 %all-to-all-done.4 = bf16[8,64,768]{2,1,0:T(8,128)(2,1)S(1)} async-done(((bf16[8,64,768]{2,1,0:T(8,128)(2,1)}), bf16[8,64,768]{2,1,0:T(8,128)(2,1)S(1)}, u32[]{:S(2)}, u32[]{:S(2)}) %all-to-all-start.4) | async-done | bytes 786464 | tf_op jit(solution)/shard_map/all_to_all | solution.py:12
  161.6 35.4 %all-gather.2.cloned.1.call-done = bf16[512,3072]{1,0:T(8,128)(2,1)} async-done(((bf16[16,3072]{1,0:T(8,128)(2,1)}), bf16[512,3072]{1,0:T(8,128)(2,1)}) %all-gather.2.cloned.1.call-update) | async-done | bytes 3145744 | tf_op jit(solution)/shard_map/all_gather | solution.py:140
  197.0 3.2 %copy.114 = bf16[3072,512]{1,0:T(8,128)(2,1)S(1)} copy(bf16[3072,512]{0,1:T(8,128)(2,1)} %bitcast.105) | data formatting | bytes 6291456 | tf_op jit(solution)/shard_map/dot_general | solution.py:139
  200.2 13.7 %convert_bitcast_fusion = bf16[96,24,32,32]{3,2,1,0:T(8,128)(2,1)} fusion(bf16[96,32,512,1]{2,1,3,0:T(8,128)(2,1)S(1)} %bitcast.106, bf16[24,32,512,1]{2,1,0,3:T(8,128)(2,1)} %bitcast.110), kind=kOutput, calls=%fused_computation.15 | convolution fusion | flops 2418278400 | bytes 8650752 | tf_op jit(solution)/shard_map/dot_general | solution.py:139
  213.9 20.1 %copy.120 = bf16[96,24,32,32]{0,3,2,1:T(8,128)(2,1)} copy(bf16[96,24,32,32]{3,2,1,0:T(8,128)(2,1)} %convert_bitcast_fusion) | data formatting | bytes 9437184 | tf_op jit(solution)/shard_map/convert_element_type | solution.py:149
  234.1 4.8 %convolution_divide_fusion = f32[96,24,128]{2,0,1:T(8,128)S(1)} fusion(bf16[96,24,1024]{0,2,1:T(8,128)(2,1)} %bitcast.98, f32[96,24]{0,1:T(8,128)S(1)} %maximum_convert_fusion, bf16[1024,128]{1,0:T(8,128)(2,1)S(1)} %copy-done), kind=kOutput, calls=%fused_computation.27 | convolution fusion | flops 604274688 | bytes 6169600 | tf_op jit(solution)/shard_map/dot_general | solution.py:151
  (89 shorter events, 43.7 us)
Async XLA Ops:
  7.2 226.9 %copy-start = (bf16[1024,128]{1,0:T(8,128)(2,1)S(1)}, bf16[1024,128]{1,0:T(8,128)(2,1)}, u32[]{:S(2)}) copy-start(bf16[1024,128]{1,0:T(8,128)(2,1)} %param.27) | copy-start | bytes 786436
  7.2 1.9 copy-start.1
  7.2 2.7 %copy-start.9 = (f32[256]{0:T(256)S(1)}, f32[256]{0:T(256)}, u32[]{:S(2)}) copy-start(f32[256]{0:T(256)} %param.18) | copy-start | bytes 3076
  9.9 7.0 %copy-start.8 = (s32[512]{0:T(512)S(1)}, s32[512]{0:T(512)}, u32[]{:S(2)}) copy-start(s32[512]{0:T(512)} %param.16) | copy-start | bytes 6148
  11.4 17.1 %all-to-all-start = ((bf16[64,8,3,256]{3,0,2,1:T(8,128)(2,1)}), bf16[64,8,3,256]{3,0,2,1:T(8,128)(2,1)S(1)}, u32[]{:S(2)}, u32[]{:S(2)}) async-start(bf16[64,8,3,256]{3,0,2,1:T(8,128)(2,1)} %bitcast.5), calls=%async_computation | async-start | bytes 1572864 | tf_op jit(solution)/shard_map/all_to_all | solution.py:73
  30.1 3.4 %copy-start.5 = (bf16[256,256]{1,0:T(8,128)(2,1)S(1)}, bf16[256,256]{1,0:T(8,128)(2,1)}, u32[]{:S(2)}) copy-start(bf16[256,256]{1,0:T(8,128)(2,1)} %param.22) | copy-start | bytes 393220
  33.9 3.5 %copy-start.6 = (bf16[256,256]{1,0:T(8,128)(2,1)S(1)}, bf16[256,256]{1,0:T(8,128)(2,1)}, u32[]{:S(2)}) copy-start(bf16[256,256]{1,0:T(8,128)(2,1)} %param.20) | copy-start | bytes 393220
  37.7 3.5 %copy-start.7 = (bf16[256,256]{1,0:T(8,128)(2,1)S(1)}, bf16[256,256]{1,0:T(8,128)(2,1)}, u32[]{:S(2)}) copy-start(bf16[256,256]{1,0:T(8,128)(2,1)} %param.21) | copy-start | bytes 393220
  42.5 4.1 %copy-start.3 = (bf16[256,256]{1,0:T(8,128)(2,1)S(1)}, bf16[256,256]{1,0:T(8,128)(2,1)}, u32[]{:S(2)}) copy-start(bf16[256,256]{1,0:T(8,128)(2,1)} %param.23) | copy-start | bytes 393220
  91.8 19.2 %all-to-all-start.1 = ((bf16[512,1,3,256]{3,2,1,0:T(4,128)(2,1)}), bf16[512,1,3,256]{3,2,1,0:T(4,128)(2,1)S(1)}, u32[]{:S(2)}, u32[]{:S(2)}) async-start(bf16[512,1,3,256]{3,2,1,0:T(4,128)(2,1)} %bitcast.102), calls=%async_computation.1 | async-start | bytes 2097152 | tf_op jit(solution)/shard_map/all_to_all | solution.py:92
  96.0 100.9 %all-gather.2.cloned.1.call-start = ((), (), s32[]{:S(2)}) async-start(), calls=%async_computation.5 | async-start | bytes 3244032 | tf_op jit(solution)/shard_map/all_gather | solution.py:140
  111.0 0.9 copy-start.4
  112.7 30.3 %copy-start.2 = (f32[64,24,256]{2,1,0:T(8,128)}, f32[64,24,256]{2,1,0:T(8,128)S(1)}, u32[]{:S(2)}) copy-start(f32[64,24,256]{2,1,0:T(8,128)S(1)} %get-tuple-element.100) | copy-start | bytes 4718596
  112.7 0.9 copy-start.10
  112.7 0.9 copy-start.12
  113.6 29.4 %copy-start.11 = (bf16[256,32]{0,1:T(8,128)(2,1)S(1)}, bf16[256,32]{0,1:T(8,128)(2,1)}, u32[]{:S(2)}) copy-start(bf16[256,32]{0,1:T(8,128)(2,1)} %param.26) | copy-start | bytes 49156
  145.3 13.7 %all-to-all-start.4 = ((bf16[8,64,768]{2,1,0:T(8,128)(2,1)}), bf16[8,64,768]{2,1,0:T(8,128)(2,1)S(1)}, u32[]{:S(2)}, u32[]{:S(2)}) async-start(bf16[8,64,768]{2,1,0:T(8,128)(2,1)} %broadcast_in_dim.23), calls=%async_computation.4 | async-start | bytes 1572864 | tf_op jit(solution)/shard_map/all_to_all | solution.py:12
Sparse Core Ops, SparseCore 0:
  143.2 53.7 all-gather.1
where the time goes:
time: 249 us; the launch traced here: 247 us
  waiting for transfers between devices  69 us (28%)
  local copies, waits for them, and re-layouts  60.3 us (24%)
  matrix products  53.5 us (21%)
  blocking collectives  27.5 us (11%)
  between operations  14.3 us (6%)
  starting transfers between devices  13.4 us (5%)
  other arithmetic  9.38 us (4%)
    all_gather x1, waiting for transfers between devices, shards(): lax.all_gather(own_block, 'col', axis=0, tiled=True)  35.4 us
    convert_element_type x1, local copies, waits for them, and re-layouts, shards(): outer_sum = products.reshape(pair_rows, side_width, res_dev, side_width)....  20.1 us
    all_to_all x1, blocking collectives, shards(): lax.all_to_all(left, 'col', split_axis=0, concat_axis=1, tiled=True)  19.5 us
    sub x3, matrix products, column(): weights = jax.nn.softmax(logits, axis=-1).astype(jnp.bfloat16)  15 us
    all_to_all x1, waiting for transfers between devices, shards(): lax.all_to_all(gated_output, 'row', split_axis=0, concat_axis=1, tiled=True)  14 us
    dot_general x1, matrix products, shards(): lax.dot_general(lax.all_gather(own_block, 'col', axis=0, tiled=True), rig...  13.7 us
    dot_general x3, matrix products, column(): jnp.einsum('hst,thd->shd', weights, heads_value, preferred_element_type=j...  12.7 us
    all_to_all x1, waiting for transfers between devices, shards(): lax.all_to_all(normed, 'row', split_axis=1, concat_axis=0, tiled=True)[:, 0]  11.5 us
  transfers between devices with their start and end apart: 4, of which 4 were waited for; matrix products, arithmetic and copies ran while one was open for 3% of the time, Pallas kernels for 0%

commit v1 on v0

--- a/solution.py
+++ b/solution.py
@@ -136,11 +136,14 @@
     )
     spread_out = lax.all_to_all(left, "col", split_axis=0, concat_axis=1, tiled=True)
     own_block = lax.all_to_all(spread_out, "row", split_axis=1, concat_axis=0, tiled=True)
+
+    def supply_all_record(inner_x, along_dim=0):
+        left_arr = lax.all_to_all(jnp.stack([inner_x] * lax.axis_size("col")), "col", 0, 0)
+        o_now = jnp.concatenate(left_arr, axis=along_dim)
+        return o_now
+
     products = lax.dot_general(
-        lax.all_gather(own_block, "col", axis=0, tiled=True),
-        right_order,
-        contraction,
-        preferred_element_type=jnp.float32,
+        supply_all_record(own_block), right_order, contraction, preferred_element_type=jnp.float32
     )
     outer_sum = (
         products.reshape(pair_rows, side_width, res_dev, side_width)

time: 249 us -> 282 us (1.13)
  the two profiles are of different devices: /device:TPU:5 before, /device:TPU:33 now
where the time goes in v1:
time: 282 us; the launch traced here: 281 us
  waiting for transfers between devices  106 us (38%)
  local copies, waits for them, and re-layouts  67.1 us (24%)
  matrix products  54.2 us (19%)
  starting transfers between devices  22.6 us (8%)
  blocking collectives  20.9 us (7%)
  other arithmetic  9.27 us (3%)
    all_to_all x1, waiting for transfers between devices, supply_all_record(): lax.all_to_all(jnp.stack([inner_x] * lax.axis_size('col')), 'col', 0, 0)  65.3 us
    all_to_all x1, blocking collectives, shards(): lax.all_to_all(left, 'col', split_axis=0, concat_axis=1, tiled=True)  20.9 us
    convert_element_type x1, local copies, waits for them, and re-layouts, shards(): outer_sum = products.reshape(pair_rows, side_width, res_dev, side_width)....  20.1 us
    sub x3, matrix products, column(): weights = jax.nn.softmax(logits, axis=-1).astype(jnp.bfloat16)  15.1 us
    dot_general x1, matrix products, shards(): lax.dot_general(supply_all_record(own_block), right_order, contraction, p...  14.4 us
    all_to_all x1, waiting for transfers between devices, shards(): lax.all_to_all(gated_output, 'row', split_axis=0, concat_axis=1, tiled=True)  13.8 us
    dot_general x3, matrix products, column(): jnp.einsum('hst,thd->shd', weights, heads_value, preferred_element_type=j...  12.7 us
    all_to_all x1, waiting for transfers between devices, shards(): lax.all_to_all(normed, 'row', split_axis=1, concat_axis=0, tiled=True)[:, 0]  11.9 us
  transfers between devices with their start and end apart: 5, of which 5 were waited for; matrix products, arithmetic and copies ran while one was open for 4% of the time, Pallas kernels for 0%

profile of v1, /device:TPU:33, one launch (start us, length us, event | category | flops | bytes accessed | tf_op | source)
XLA Modules:
  0.0 280.6 jit_solution(15213163013874136830)
XLA Ops:
  4.9 5.4 %all-to-all-start = ((bf16[64,8,3,256]{3,0,2,1:T(8,128)(2,1)}), bf16[64,8,3,256]{3,0,2,1:T(8,128)(2,1)S(1)}, u32[]{:S(2)}, u32[]{:S(2)}) async-start(bf16[64,8,3,256]{3,0,2,1:T(8,128)(2,1)} %bitcast.5), calls=%async_computation | async-start | bytes 1572864 | tf_op jit(solution)/shard_map/all_to_all | solution.py:73
  10.2 11.9 %all-to-all-done = bf16[64,8,3,256]{3,0,2,1:T(8,128)(2,1)S(1)} async-done(((bf16[64,8,3,256]{3,0,2,1:T(8,128)(2,1)}), bf16[64,8,3,256]{3,0,2,1:T(8,128)(2,1)S(1)}, u32[]{:S(2)}, u32[]{:S(2)}) %all-to-all-start) | async-done | bytes 786464 | tf_op jit(solution)/shard_map/all_to_all | solution.py:73
  40.2 2.6 convolution_bitcast_fusion
  42.9 40.3 %while.10 = (s32[]{:T(128)}, bf16[3,512,256]{1,2,0:T(8,128)(2,1)}, f32[3,512,256]{2,1,0:T(8,128)}, bf16[3,512,256]{1,2,0:T(8,128)(2,1)}, bf16[3,512,256]{1,2,0:T...) while((s32[]{:T(128)}, bf16[3,512,256]{1,2,0:T(8,128)(2,1)}, ...), condition=%wide.region_5.6_spmd, body=%wide.region_2.5_spmd.sunk | while | flops 279577088 | bytes 23104096 | solution.py:88
  43.9 5.0 %fusion.43 = (f32[8,512]{1,0:T(8,128)S(1)}, f32[8,512,512]{1,2,0:T(8,128)}) fusion(f32[512]{0:T(512)S(1)} %get-tuple-element.174, bf16[512,8,32]{0,2,1:T(8,128)(2,1)S(1)} %bitcast.100, bf16[512,8,32]{0,2,1:T(8,128)(2,1)S(1)} %bitcast.99), kind=kOutput, calls=%fused_computation.46.clone.1 | convolution fusion | flops 140509696 | bytes 8931328 | tf_op jit(solution)/shard_map/while/body/eval_jaxpr/sub | solution.py:67
  49.9 4.2 %fusion.44 = f32[8,32,512]{2,1,0:T(8,128)S(1)} fusion(bf16[512,8,32]{0,2,1:T(8,128)(2,1)S(1)} %bitcast.98, f32[8,512,512]{1,2,0:T(8,128)} %get-tuple-element.150, f32[8,512]{1,0:T(8,128)S(1)} %get-tuple-element.151), kind=kOutput, calls=%fused_computation.6.clone.1 | convolution fusion | flops 138412032 | bytes 9191424 | tf_op jit(solution)/shard_map/while/body/eval_jaxpr/hst,thd->shd/dot_general | solution.py:68
  57.4 5.0 %fusion.43 = (f32[8,512]{1,0:T(8,128)S(1)}, f32[8,512,512]{1,2,0:T(8,128)}) fusion(f32[512]{0:T(512)S(1)} %get-tuple-element.174, bf16[512,8,32]{0,2,1:T(8,128)(2,1)S(1)} %bitcast.100, bf16[512,8,32]{0,2,1:T(8,128)(2,1)S(1)} %bitcast.99), kind=kOutput, calls=%fused_computation.46.clone.1 | convolution fusion | flops 140509696 | bytes 8931328 | tf_op jit(solution)/shard_map/while/body/eval_jaxpr/sub | solution.py:67
  63.4 4.2 %fusion.44 = f32[8,32,512]{2,1,0:T(8,128)S(1)} fusion(bf16[512,8,32]{0,2,1:T(8,128)(2,1)S(1)} %bitcast.98, f32[8,512,512]{1,2,0:T(8,128)} %get-tuple-element.150, f32[8,512]{1,0:T(8,128)S(1)} %get-tuple-element.151), kind=kOutput, calls=%fused_computation.6.clone.1 | convolution fusion | flops 138412032 | bytes 9191424 | tf_op jit(solution)/shard_map/while/body/eval_jaxpr/hst,thd->shd/dot_general | solution.py:68
  70.8 5.0 %fusion.43 = (f32[8,512]{1,0:T(8,128)S(1)}, f32[8,512,512]{1,2,0:T(8,128)}) fusion(f32[512]{0:T(512)S(1)} %get-tuple-element.174, bf16[512,8,32]{0,2,1:T(8,128)(2,1)S(1)} %bitcast.100, bf16[512,8,32]{0,2,1:T(8,128)(2,1)S(1)} %bitcast.99), kind=kOutput, calls=%fused_computation.46.clone.1 | convolution fusion | flops 140509696 | bytes 8931328 | tf_op jit(solution)/shard_map/while/body/eval_jaxpr/sub | solution.py:67
  76.8 4.2 %fusion.44 = f32[8,32,512]{2,1,0:T(8,128)S(1)} fusion(bf16[512,8,32]{0,2,1:T(8,128)(2,1)S(1)} %bitcast.98, f32[8,512,512]{1,2,0:T(8,128)} %get-tuple-element.150, f32[8,512]{1,0:T(8,128)S(1)} %get-tuple-element.151), kind=kOutput, calls=%fused_computation.6.clone.1 | convolution fusion | flops 138412032 | bytes 9191424 | tf_op jit(solution)/shard_map/while/body/eval_jaxpr/hst,thd->shd/dot_general | solution.py:68
  85.5 3.9 %all-to-all-start.1 = ((bf16[512,1,3,256]{3,2,1,0:T(4,128)(2,1)}), bf16[512,1,3,256]{3,2,1,0:T(4,128)(2,1)S(1)}, u32[]{:S(2)}, u32[]{:S(2)}) async-start(bf16[512,1,3,256]{3,2,1,0:T(4,128)(2,1)} %bitcast.105), calls=%async_computation.1 | async-start | bytes 2097152 | tf_op jit(solution)/shard_map/all_to_all | solution.py:92
  90.3 13.8 %all-to-all-done.1 = bf16[512,1,3,256]{3,2,1,0:T(4,128)(2,1)S(1)} async-done(((bf16[512,1,3,256]{3,2,1,0:T(4,128)(2,1)}), bf16[512,1,3,256]{3,2,1,0:T(4,128)(2,1)S(1)}, u32[]{:S(2)}, u32[]{:S(2)}) %all-to-all-start.1) | async-done | bytes 786464 | tf_op jit(solution)/shard_map/all_to_all | solution.py:92
  107.9 20.9 %all_to_all.72 = bf16[32,2,768]{2,1,0:T(2,128)(2,1)} all-to-all(bf16[32,2,768]{2,1,0:T(2,128)(2,1)S(1)} %all_to_all.58), channel_id=1, replica_groups=mesh['row'=8,'col'=32] {'col'}, dimensions={0} | all-to-all | bytes 196608 | tf_op jit(solution)/shard_map/all_to_all | solution.py:137
  128.9 4.2 %all-to-all-start.3 = ((bf16[2,8,3072]{2,0,1:T(2,128)(2,1)}), bf16[2,8,3072]{2,0,1:T(2,128)(2,1)S(1)}, u32[]{:S(2)}, u32[]{:S(2)}) async-start(bf16[2,8,3072]{2,0,1:T(2,128)(2,1)} %bitcast.23), calls=%async_computation.3 | async-start | bytes 196608 | tf_op jit(solution)/shard_map/all_to_all | solution.py:138
  134.3 2.9 %all-to-all-done.3 = bf16[2,8,3072]{2,0,1:T(2,128)(2,1)S(1)} async-done(((bf16[2,8,3072]{2,0,1:T(2,128)(2,1)}), bf16[2,8,3072]{2,0,1:T(2,128)(2,1)S(1)}, u32[]{:S(2)}, u32[]{:S(2)}) %all-to-all-start.3) | async-done | bytes 98336 | tf_op jit(solution)/shard_map/all_to_all | solution.py:138
  138.2 4.6 %all-to-all-start.5 = ((bf16[8,64,768]{2,1,0:T(8,128)(2,1)}), bf16[8,64,768]{2,1,0:T(8,128)(2,1)S(1)}, u32[]{:S(2)}, u32[]{:S(2)}) async-start(bf16[8,64,768]{2,1,0:T(8,128)(2,1)} %broadcast_in_dim.23), calls=%async_computation.5 | async-start | bytes 1572864 | tf_op jit(solution)/shard_map/all_to_all | solution.py:12
  142.8 11.9 %all-to-all-done.5 = bf16[8,64,768]{2,1,0:T(8,128)(2,1)S(1)} async-done(((bf16[8,64,768]{2,1,0:T(8,128)(2,1)}), bf16[8,64,768]{2,1,0:T(8,128)(2,1)S(1)}, u32[]{:S(2)}, u32[]{:S(2)}) %all-to-all-start.5) | async-done | bytes 786464 | tf_op jit(solution)/shard_map/all_to_all | solution.py:12
  156.7 4.5 %all-to-all-start.4 = ((bf16[32,16,3072]{2,1,0:T(8,128)(2,1)}), bf16[32,16,3072]{2,1,0:T(8,128)(2,1)S(1)}, u32[]{:S(2)}, u32[]{:S(2)}) async-start(bf16[32,16,3072]{2,1,0:T(8,128)(2,1)} %stack.5), calls=%async_computation.4 | async-start | bytes 6291456 | tf_op jit(solution)/shard_map/all_to_all | solution.py:141
  166.3 2.9 %reshape.168 = bf16[512,768]{1,0:T(8,128)(2,1)} reshape(bf16[32,8,2,768]{3,2,1,0:T(2,128)(2,1)} %copy.118) | data formatting | bytes 1572864 | tf_op jit(solution)/shard_map/reshape | solution.py:135
  171.5 65.3 %all-to-all-done.4 = bf16[32,16,3072]{2,1,0:T(8,128)(2,1)S(1)} async-done(((bf16[32,16,3072]{2,1,0:T(8,128)(2,1)}), bf16[32,16,3072]{2,1,0:T(8,128)(2,1)S(1)}, u32[]{:S(2)}, u32[]{:S(2)}) %all-to-all-start.4) | async-done | bytes 3145760 | tf_op jit(solution)/shard_map/all_to_all | solution.py:141
  236.8 2.8 copy.114
  239.6 14.4 %convert_bitcast_fusion = bf16[96,24,32,32]{3,2,1,0:T(8,128)(2,1)} fusion(bf16[96,32,512,1]{2,1,3,0:T(8,128)(2,1)} %bitcast.108, bf16[24,32,512,1]{2,1,0,3:T(8,128)(2,1)} %bitcast.112), kind=kOutput, calls=%fused_computation.15 | convolution fusion | flops 2418278400 | bytes 8650752 | tf_op jit(solution)/shard_map/dot_general | solution.py:145
  254.0 20.1 %copy.120 = bf16[96,24,32,32]{0,3,2,1:T(8,128)(2,1)} copy(bf16[96,24,32,32]{3,2,1,0:T(8,128)(2,1)} %convert_bitcast_fusion) | data formatting | bytes 9437184 | tf_op jit(solution)/shard_map/convert_element_type | solution.py:152
  274.1 4.8 %convolution_divide_fusion = f32[96,24,128]{2,0,1:T(8,128)S(1)} fusion(bf16[96,24,1024]{0,2,1:T(8,128)(2,1)} %bitcast.101, f32[96,24]{0,1:T(8,128)S(1)} %maximum_convert_fusion, bf16[1024,128]{1,0:T(8,128)(2,1)S(1)} %copy-done), kind=kOutput, calls=%fused_computation.27 | convolution fusion | flops 604274688 | bytes 6169600 | tf_op jit(solution)/shard_map/dot_general | solution.py:154
  (92 shorter events, 55.0 us)
Async XLA Ops:
  0.6 273.5 %copy-start = (bf16[1024,128]{1,0:T(8,128)(2,1)S(1)}, bf16[1024,128]{1,0:T(8,128)(2,1)}, u32[]{:S(2)}) copy-start(bf16[1024,128]{1,0:T(8,128)(2,1)} %param.27) | copy-start | bytes 786436
  0.6 1.9 copy-start.1
  0.7 2.7 copy-start.10
  3.4 6.9 %copy-start.9 = (s32[512]{0:T(512)S(1)}, s32[512]{0:T(512)}, u32[]{:S(2)}) copy-start(s32[512]{0:T(512)} %param.16) | copy-start | bytes 6148
  4.9 17.2 %all-to-all-start = ((bf16[64,8,3,256]{3,0,2,1:T(8,128)(2,1)}), bf16[64,8,3,256]{3,0,2,1:T(8,128)(2,1)S(1)}, u32[]{:S(2)}, u32[]{:S(2)}) async-start(bf16[64,8,3,256]{3,0,2,1:T(8,128)(2,1)} %bitcast.5), calls=%async_computation | async-start | bytes 1572864 | tf_op jit(solution)/shard_map/all_to_all | solution.py:73
  23.8 3.4 %copy-start.6 = (bf16[256,256]{1,0:T(8,128)(2,1)S(1)}, bf16[256,256]{1,0:T(8,128)(2,1)}, u32[]{:S(2)}) copy-start(bf16[256,256]{1,0:T(8,128)(2,1)} %param.22) | copy-start | bytes 393220
  27.5 3.5 %copy-start.7 = (bf16[256,256]{1,0:T(8,128)(2,1)S(1)}, bf16[256,256]{1,0:T(8,128)(2,1)}, u32[]{:S(2)}) copy-start(bf16[256,256]{1,0:T(8,128)(2,1)} %param.20) | copy-start | bytes 393220
  31.4 3.5 %copy-start.8 = (bf16[256,256]{1,0:T(8,128)(2,1)S(1)}, bf16[256,256]{1,0:T(8,128)(2,1)}, u32[]{:S(2)}) copy-start(bf16[256,256]{1,0:T(8,128)(2,1)} %param.21) | copy-start | bytes 393220
  36.1 4.1 %copy-start.4 = (bf16[256,256]{1,0:T(8,128)(2,1)S(1)}, bf16[256,256]{1,0:T(8,128)(2,1)}, u32[]{:S(2)}) copy-start(bf16[256,256]{1,0:T(8,128)(2,1)} %param.23) | copy-start | bytes 393220
  85.5 18.6 %all-to-all-start.1 = ((bf16[512,1,3,256]{3,2,1,0:T(4,128)(2,1)}), bf16[512,1,3,256]{3,2,1,0:T(4,128)(2,1)S(1)}, u32[]{:S(2)}, u32[]{:S(2)}) async-start(bf16[512,1,3,256]{3,2,1,0:T(4,128)(2,1)} %bitcast.105), calls=%async_computation.1 | async-start | bytes 2097152 | tf_op jit(solution)/shard_map/all_to_all | solution.py:92
  104.1 0.9 copy-start.5
  105.8 27.2 %copy-start.2 = (f32[64,24,256]{2,1,0:T(8,128)}, f32[64,24,256]{2,1,0:T(8,128)S(1)}, u32[]{:S(2)}) copy-start(f32[64,24,256]{2,1,0:T(8,128)S(1)} %get-tuple-element.100) | copy-start | bytes 4718596
  105.8 0.9 copy-start.11
  105.8 0.9 copy-start.13
  106.5 26.5 %copy-start.12 = (bf16[256,32]{0,1:T(8,128)(2,1)S(1)}, bf16[256,32]{0,1:T(8,128)(2,1)}, u32[]{:S(2)}) copy-start(bf16[256,32]{0,1:T(8,128)(2,1)} %param.26) | copy-start | bytes 49156
  128.9 8.4 %all-to-all-start.3 = ((bf16[2,8,3072]{2,0,1:T(2,128)(2,1)}), bf16[2,8,3072]{2,0,1:T(2,128)(2,1)S(1)}, u32[]{:S(2)}, u32[]{:S(2)}) async-start(bf16[2,8,3072]{2,0,1:T(2,128)(2,1)} %bitcast.23), calls=%async_computation.3 | async-start | bytes 196608 | tf_op jit(solution)/shard_map/all_to_all | solution.py:138
  138.2 16.5 %all-to-all-start.5 = ((bf16[8,64,768]{2,1,0:T(8,128)(2,1)}), bf16[8,64,768]{2,1,0:T(8,128)(2,1)S(1)}, u32[]{:S(2)}, u32[]{:S(2)}) async-start(bf16[8,64,768]{2,1,0:T(8,128)(2,1)} %broadcast_in_dim.23), calls=%async_computation.5 | async-start | bytes 1572864 | tf_op jit(solution)/shard_map/all_to_all | solution.py:12
  154.7 2.0 copy-start.3
  156.7 80.1 %all-to-all-start.4 = ((bf16[32,16,3072]{2,1,0:T(8,128)(2,1)}), bf16[32,16,3072]{2,1,0:T(8,128)(2,1)S(1)}, u32[]{:S(2)}, u32[]{:S(2)}) async-start(bf16[32,16,3072]{2,1,0:T(8,128)(2,1)} %stack.5), calls=%async_computation.4 | async-start | bytes 6291456 | tf_op jit(solution)/shard_map/all_to_all | solution.py:141
